TPU v7x, 32 devices: a whole 2x2x4 slice. The times are simulated.
32 devices in a mesh: bank: 4 (over z), zero: 8 (over y, x, core).
Axes of the slice: x: 2, y: 2, z: 4, core: 2. Of those that a mesh axis runs over, the one named last changes fastest.
Arguments:
- w_gate: float32 [128, 2048, 768], P('bank', 'zero'), may hold values from -0.1875 to 0.1875
- w_up: float32 [128, 2048, 768], P('bank', 'zero'), may hold values from -0.1875 to 0.1875
- router_weight: float32 [2048, 128], P('zero', 'bank'), may hold values from -0.125 to 0.125
- router_gain: float32 [2048], P('zero'), may hold values from 0.25 to 1.75
Outputs:
- serve_gate: bfloat16 [128, 2048, 768], P('bank', None, 'zero')
- serve_up: bfloat16 [128, 2048, 768], P('bank', None, 'zero')
- scale_gate: float32 [128, 768], P('bank', 'zero')
- scale_up: float32 [128, 768], P('bank', 'zero')
- serve_router: bfloat16 [2048, 128], replicated
All inputs are finite; a program needn't handle non-finite values.
Results may differ from a plain program's by a relative error of at most 0.001.
Values may be sent and summed in bfloat16 or wider, within the bound.
A program may use at most 192 MiB of HBM per device.

v0:
```python
import jax
import jax.numpy as jnp
from jax import lax
from jax.sharding import PartitionSpec as P


def shards(w_gate, w_up, router_weight, router_gain):
    total_gate, total_up = lax.psum(
        (jnp.sum(w_gate * w_gate, axis=1), jnp.sum(w_up * w_up, axis=1)), "zero"
    )
    scale_gate = jnp.sqrt(total_gate)
    scale_up = jnp.sqrt(total_up)
    narrow_gate, narrow_up = (
        (w_gate / jnp.expand_dims(scale_gate, 1)).astype(jnp.bfloat16),
        (w_up / jnp.expand_dims(scale_up, 1)).astype(jnp.bfloat16),
    )
    serve_gate, serve_up = (
        lax.all_to_all(narrow_gate, "zero", split_axis=2, concat_axis=1, tiled=True),
        lax.all_to_all(narrow_up, "zero", split_axis=2, concat_axis=1, tiled=True),
    )
    scale_gate = lax.dynamic_slice_in_dim(
        scale_gate, lax.axis_index("zero") * serve_gate.shape[2], serve_gate.shape[2], axis=1
    )
    scale_up = lax.dynamic_slice_in_dim(
        scale_up, lax.axis_index("zero") * serve_up.shape[2], serve_up.shape[2], axis=1
    )
    part_router = (router_weight * router_gain[:, None]).astype(jnp.bfloat16)
    row_router = lax.all_gather(part_router, "zero", axis=0, tiled=True)
    serve_router = lax.all_gather(row_router, "bank", axis=1, tiled=True)
    return (serve_gate, serve_up, scale_gate, scale_up, serve_router)


def solution(mesh):
    placed = (P("bank", "zero", None), P("bank", "zero", None), P("zero", "bank"), P("zero"))
    return jax.shard_map(
        shards,
        mesh=mesh,
        in_specs=placed,
        out_specs=(
            P("bank", None, "zero"),
            P("bank", None, "zero"),
            P("bank", "zero"),
            P("bank", "zero"),
            P(),
        ),
        check_vma=False,
    )
```

profile of v0, /device:TPU:0, one launch (start us, length us, event | category | flops | bytes accessed | tf_op | source)
XLA Modules:
  0.0 481.0 jit_solution(10650282860068963028)
XLA Ops:
  7.2 0.0 all-reduce.3.cloned.1.call-start
  7.2 17.3 %multiply_reduce_fusion = (f32[32,768]{1,0:T(8,128)}, f32[32,768]{1,0:T(8,128)}) fusion(f32[32,256,768]{2,1,0:T(8,128)} %param.5, f32[32,256,768]{2,1,0:T(8,128)} %param.4), kind=kLoop, calls=%fused_computation.1 | loop fusion | flops 25116672 | bytes 50528256 | tf_op jit(solution)/shard_map/reduce_sum | solution.py:9
  24.5 0.0 all-reduce.3.cloned.1.call-update
  24.5 25.1 %copy.25 = f32[32,256,768]{1,0,2:T(8,128)} copy(f32[32,256,768]{2,1,0:T(8,128)} %param.5) | data formatting | bytes 50331648 | tf_op args[1]
  49.6 31.5 %all-reduce.3.cloned.1.call-done = (f32[32,768]{1,0:T(8,128)}, f32[32,768]{1,0:T(8,128)}) async-done(((f32[32,768]{1,0:T(8,128)}, f32[32,768]{1,0:T(8,128)}), (f32[32,768]{1,0:T(8,128)}, f32[32,768]{1,0:T(8,128)})) %all-reduce.3.cloned.1.call-update) | async-done | bytes 196624 | tf_op jit(solution)/shard_map/psum | solution.py:8
  81.1 0.9 sqrt.7
  82.1 0.2 copy.24
  82.2 14.1 %divide_convert_fusion = bf16[32,256,768]{1,0,2:T(8,128)(2,1)} fusion(f32[32,256,768]{1,0,2:T(8,128)} %copy.25, f32[32,768]{0,1:T(8,128)S(1)} %copy.24), kind=kLoop, calls=%fused_computation | loop fusion | flops 12582912 | bytes 37847040 | tf_op jit(solution)/shard_map/convert_element_type | solution.py:15
  96.4 5.4 %all-to-all-start.1 = ((bf16[32,256,768]{1,0,2:T(8,128)(2,1)}), bf16[32,256,768]{1,0,2:T(8,128)(2,1)}, u32[]{:S(2)}, u32[]{:S(2)}) async-start(bf16[32,256,768]{1,0,2:T(8,128)(2,1)} %divide_convert_fusion), calls=%async_computation.1 | async-start | bytes 25165824 | tf_op jit(solution)/shard_map/all_to_all | solution.py:19
  101.8 0.0 copy-start
  101.8 25.1 %copy.21 = f32[32,256,768]{1,0,2:T(8,128)} copy(f32[32,256,768]{2,1,0:T(8,128)} %param.4) | data formatting | bytes 50331648 | tf_op args[0]
  126.9 0.0 copy-done
  126.9 0.2 copy.20
  127.1 0.0 copy-start.1
  127.1 0.0 copy-start.2
  127.1 14.1 %divide_convert_fusion.1 = bf16[32,256,768]{1,0,2:T(8,128)(2,1)} fusion(f32[32,256,768]{1,0,2:T(8,128)} %copy.21, f32[32,768]{0,1:T(8,128)S(1)} %copy.20), kind=kLoop, calls=%fused_computation.2 | loop fusion | flops 12582912 | bytes 37847040 | tf_op jit(solution)/shard_map/convert_element_type | solution.py:14
  141.3 99.5 %all-to-all-done.1 = bf16[32,256,768]{1,0,2:T(8,128)(2,1)} async-done(((bf16[32,256,768]{1,0,2:T(8,128)(2,1)}), bf16[32,256,768]{1,0,2:T(8,128)(2,1)}, u32[]{:S(2)}, u32[]{:S(2)}) %all-to-all-start.1) | async-done | bytes 12582944 | tf_op jit(solution)/shard_map/all_to_all | solution.py:19
  240.8 5.4 %all-to-all-start = ((bf16[32,256,768]{1,0,2:T(8,128)(2,1)}), bf16[32,256,768]{1,0,2:T(8,128)(2,1)}, u32[]{:S(2)}, u32[]{:S(2)}) async-start(bf16[32,256,768]{1,0,2:T(8,128)(2,1)} %divide_convert_fusion.1), calls=%async_computation | async-start | bytes 25165824 | tf_op jit(solution)/shard_map/all_to_all | solution.py:18
  246.1 0.0 copy-done.1
  246.1 0.0 copy-done.2
  246.2 142.4 %all_gather.6 = bf16[2048,32]{0,1:T(8,128)(2,1)S(1)} all-gather(bf16[256,32]{0,1:T(8,128)(2,1)S(1)} %multiply_convert_fusion), channel_id=1, replica_groups=mesh['bank'=4,'zero'=8] {'zero'}, dimensions={0}, use_global_device_ids=true | all-gather | bytes 147456 | tf_op jit(solution)/shard_map/all_gather | solution.py:28
  388.6 16.1 %all_gather.7 = bf16[2048,128]{0,1:T(8,128)(2,1)S(1)} all-gather(bf16[2048,32]{0,1:T(8,128)(2,1)S(1)} %all_gather.6), channel_id=1, replica_groups=mesh['bank'=4,'zero'=8] {'bank'}, dimensions={1}, use_global_device_ids=true | all-gather | bytes 655360 | tf_op jit(solution)/shard_map/all_gather | solution.py:29
  404.6 1.0 copy.28
  405.6 0.7 constant_dynamic-slice_fusion
  406.3 0.7 constant_dynamic-slice_fusion.1
  407.0 14.1 %copy.27 = bf16[32,8,256,96]{2,1,3,0:T(8,128)(2,1)} copy(bf16[32,8,256,96]{2,0,3,1:T(8,128)(2,1)} %bitcast.5) | data formatting | bytes 25165824 | tf_op jit(solution)/shard_map/all_to_all | solution.py:19
  421.1 19.5 %all_to_all.33 = bf16[32,2048,96]{1,2,0:T(8,128)(2,1)} reshape(bf16[32,8,256,96]{2,1,3,0:T(8,128)(2,1)} %copy.27) | data formatting | bytes 25165824 | tf_op jit(solution)/shard_map/all_to_all | solution.py:19
  440.6 0.0 all-to-all-done
  440.6 14.1 %copy.23 = bf16[32,8,256,96]{2,1,3,0:T(8,128)(2,1)} copy(bf16[32,8,256,96]{2,0,3,1:T(8,128)(2,1)} %bitcast.2) | data formatting | bytes 25165824 | tf_op jit(solution)/shard_map/all_to_all | solution.py:18
  454.7 19.5 %all_to_all.29 = bf16[32,2048,96]{1,2,0:T(8,128)(2,1)} reshape(bf16[32,8,256,96]{2,1,3,0:T(8,128)(2,1)} %copy.23) | data formatting | bytes 25165824 | tf_op jit(solution)/shard_map/all_to_all | solution.py:18
  (2 shorter events, 0.0 us)
Async XLA Ops:
  7.2 74.0 %all-reduce.3.cloned.1.call-start = ((), (), s32[]{:S(2)}) async-start(), calls=%async_computation.2 | async-start | bytes 393216 | tf_op jit(solution)/shard_map/psum | solution.py:8
  96.4 144.4 %all-to-all-start.1 = ((bf16[32,256,768]{1,0,2:T(8,128)(2,1)}), bf16[32,256,768]{1,0,2:T(8,128)(2,1)}, u32[]{:S(2)}, u32[]{:S(2)}) async-start(bf16[32,256,768]{1,0,2:T(8,128)(2,1)} %divide_convert_fusion), calls=%async_computation.1 | async-start | bytes 25165824 | tf_op jit(solution)/shard_map/all_to_all | solution.py:19
  101.8 25.1 %copy-start = (f32[32,768]{1,0:T(8,128)S(1)}, f32[32,768]{1,0:T(8,128)}, u32[]{:S(2)}) copy-start(f32[32,768]{1,0:T(8,128)} %get-tuple-element.10) | copy-start | bytes 294916
  127.1 119.0 %copy-start.1 = (f32[256,32]{0,1:T(8,128)S(1)}, f32[256,32]{0,1:T(8,128)}, u32[]{:S(2)}) copy-start(f32[256,32]{0,1:T(8,128)} %param.6) | copy-start | bytes 98308
  127.1 119.0 %copy-start.2 = (f32[256]{0:T(256)S(1)}, f32[256]{0:T(256)}, u32[]{:S(2)}) copy-start(f32[256]{0:T(256)} %param.7) | copy-start | bytes 3076
  240.8 199.8 %all-to-all-start = ((bf16[32,256,768]{1,0,2:T(8,128)(2,1)}), bf16[32,256,768]{1,0,2:T(8,128)(2,1)}, u32[]{:S(2)}, u32[]{:S(2)}) async-start(bf16[32,256,768]{1,0,2:T(8,128)(2,1)} %divide_convert_fusion.1), calls=%async_computation | async-start | bytes 25165824 | tf_op jit(solution)/shard_map/all_to_all | solution.py:18
Sparse Core Ops, SparseCore 0:
  24.6 56.4 all-reduce.2
where the time goes:
time: 483 us; the launch traced here: 481 us
  blocking collectives  158 us (33%)
  waiting for transfers between devices  131 us (27%)
  local copies, waits for them, and re-layouts  121 us (25%)
  other arithmetic  45.5 us (9%)
  between operations  14.1 us (3%)
  starting transfers between devices  10.8 us (2%)
    all_gather x1, blocking collectives, shards(): row_router = lax.all_gather(part_router, 'zero', axis=0, tiled=True)  142 us
    all_to_all x1, waiting for transfers between devices, shards(): lax.all_to_all(narrow_up, 'zero', split_axis=2, concat_axis=1, tiled=True)  99.5 us
    unnamed x9, local copies, waits for them, and re-layouts  51.3 us
    all_to_all x2, local copies, waits for them, and re-layouts, shards(): lax.all_to_all(narrow_gate, 'zero', split_axis=2, concat_axis=1, tiled=True)  33.6 us
    all_to_all x2, local copies, waits for them, and re-layouts, shards(): lax.all_to_all(narrow_up, 'zero', split_axis=2, concat_axis=1, tiled=True)  33.6 us
    psum x1, waiting for transfers between devices, shards(): lax.psum((jnp.sum(w_gate * w_gate, axis=1), jnp.sum(w_up * w_up, axis=1))...  31.5 us
    reduce_sum x1, other arithmetic, shards(): jnp.sum(w_up * w_up, axis=1)  17.3 us
    all_gather x1, blocking collectives, shards(): serve_router = lax.all_gather(row_router, 'bank', axis=1, tiled=True)  16.1 us
  transfers between devices with their start and end apart: 3, of which 2 were waited for; matrix products, arithmetic and copies ran while one was open for 17% of the time, Pallas kernels for 0%

commit v1 on v0

v1 whole, which is shorter than its diff:
```python
import functools

import jax
import jax.numpy as jnp
from jax import lax
from jax.experimental import pallas as pl
from jax.experimental.pallas import tpu as pltpu
from jax.sharding import PartitionSpec as P


def prepare_kernel(parts, w_ref, scale_ref, out_ref):
    normal = w_ref[0] / scale_ref[0]
    turned = normal.T
    width = turned.shape[0] // parts
    for part in range(parts):
        out_ref[part, 0] = turned[part * width : (part + 1) * width].astype(jnp.bfloat16)


def prepare(w, scale, parts, first, count):
    _, rows, columns = w.shape
    width = columns // parts
    return pl.pallas_call(
        functools.partial(prepare_kernel, parts),
        grid=(count,),
        in_specs=[
            pl.BlockSpec((1, rows, columns), lambda e: (e + first, 0, 0)),
            pl.BlockSpec((1, 1, columns), lambda e: (e + first, 0, 0)),
        ],
        out_specs=pl.BlockSpec((parts, 1, width, rows), lambda e: (0, e, 0, 0)),
        out_shape=jax.ShapeDtypeStruct((parts, count, width, rows), jnp.bfloat16),
        cost_estimate=pl.CostEstimate(
            flops=count * rows * columns * 40,
            bytes_accessed=count * rows * columns * 6,
            transcendentals=0,
        ),
        compiler_params=pltpu.CompilerParams(vmem_limit_bytes=32 * 2**20),
        name="prepare",
    )(w, scale[:, None, :])


def merge_kernel(parts, block_ref, *refs):
    out_ref = refs[-1]
    rows = block_ref.shape[3]
    for part in range(parts):
        out_ref[0, :, part * rows : (part + 1) * rows] = block_ref[part, 0]


def merge(blocks, before, experts, first):
    parts, count, width, rows = blocks.shape
    chained = before is not None
    return pl.pallas_call(
        functools.partial(merge_kernel, parts),
        grid=(count,),
        in_specs=[pl.BlockSpec((parts, 1, width, rows), lambda e: (0, e, 0, 0))]
        + [pl.BlockSpec(memory_space=pl.ANY)] * chained,
        out_specs=pl.BlockSpec((1, width, parts * rows), lambda e: (e + first, 0, 0)),
        out_shape=jax.ShapeDtypeStruct((experts, width, parts * rows), jnp.bfloat16),
        input_output_aliases={1: 0} if chained else {},
        cost_estimate=pl.CostEstimate(
            flops=count * rows * width * parts * 10,
            bytes_accessed=count * rows * width * parts * 4,
            transcendentals=0,
        ),
        compiler_params=pltpu.CompilerParams(vmem_limit_bytes=32 * 2**20),
        name="merge",
    )(blocks, *([before] if chained else []))


def cuts(experts, small_first):
    small = max(experts // 4, 1)
    sizes = [small, experts - small] if small_first else [experts - small, small]
    return [size for size in sizes if size]


def shards_blocked(parts, w_gate, w_up, router_weight, router_gain):
    experts, rows, columns = w_gate.shape
    width = columns // parts
    sums = jnp.stack(
        [jnp.sum(w_gate * w_gate, axis=1), jnp.sum(w_up * w_up, axis=1)]
    ).reshape(2 * experts, parts, width)
    pieces = lax.all_to_all(
        sums.transpose(1, 0, 2), "zero", split_axis=0, concat_axis=0, tiled=True
    )
    own = jnp.sqrt(jnp.sum(pieces, axis=0))
    scale_gate, scale_up = own[:experts], own[experts:]

    part_router = (router_weight * router_gain[:, None]).astype(jnp.bfloat16)
    packed = jnp.concatenate(
        [own.reshape(-1), part_router.astype(jnp.float32).reshape(-1)]
    ).reshape(1, -1, 128)
    gathered = lax.all_gather(packed, "zero", axis=0, tiled=True).reshape(parts, -1)
    scales = gathered[:, : own.size].reshape(parts, 2 * experts, width)
    scales = scales.transpose(1, 0, 2).reshape(2 * experts, columns)
    row_router = gathered[:, own.size :].reshape(parts * rows, -1).astype(jnp.bfloat16)

    results, last = [], None
    for w, scale, small_first in ((w_gate, scales[:experts], True), (w_up, scales[experts:], False)):
        first, result = 0, None
        for count in cuts(experts, small_first):
            last = prepare(w, scale, parts, first, count)
            blocks = lax.all_to_all(last, "zero", split_axis=0, concat_axis=0, tiled=True)
            result = merge(blocks, result, experts, first)
            first += count
        results.append(result.transpose(0, 2, 1))
    row_router, _ = lax.optimization_barrier((row_router, last))
    serve_router = lax.all_gather(row_router, "bank", axis=1, tiled=True)
    return (*results, scale_gate, scale_up, serve_router)


def shards_plain(w_gate, w_up, router_weight, router_gain):
    total_gate, total_up = lax.psum(
        (jnp.sum(w_gate * w_gate, axis=1), jnp.sum(w_up * w_up, axis=1)), "zero"
    )
    results, own = [], []
    for w, total in ((w_gate, total_gate), (w_up, total_up)):
        scale = jnp.sqrt(total)
        narrow = (w / jnp.expand_dims(scale, 1)).astype(jnp.bfloat16)
        serve = lax.all_to_all(narrow, "zero", split_axis=2, concat_axis=1, tiled=True)
        width = serve.shape[2]
        results.append(serve)
        own.append(
            lax.dynamic_slice_in_dim(scale, lax.axis_index("zero") * width, width, axis=1)
        )
    part_router = (router_weight * router_gain[:, None]).astype(jnp.bfloat16)
    row_router = lax.all_gather(part_router, "zero", axis=0, tiled=True)
    serve_router = lax.all_gather(row_router, "bank", axis=1, tiled=True)
    return (*results, *own, serve_router)


def solution(mesh):
    parts, banks = mesh.shape["zero"], mesh.shape["bank"]
    placed = (P("bank", "zero", None), P("bank", "zero", None), P("zero", "bank"), P("zero"))

    def shards(w_gate, w_up, router_weight, router_gain):
        experts, rows, columns = w_gate.shape
        width = columns // parts
        packed = 2 * experts * width + router_weight.size
        if rows % 128 == 0 and width % 16 == 0 and packed % 128 == 0:
            return shards_blocked(parts, w_gate, w_up, router_weight, router_gain)
        return shards_plain(w_gate, w_up, router_weight, router_gain)

    return jax.shard_map(
        shards,
        mesh=mesh,
        in_specs=placed,
        out_specs=(
            P("bank", None, "zero"),
            P("bank", None, "zero"),
            P("bank", "zero"),
            P("bank", "zero"),
            P(),
        ),
        check_vma=False,
    )
```

time: 483 us -> 380 us (0.79)
  blocking collectives: 158 us -> 25.6 us
  local copies, waits for them, and re-layouts: 121 us -> 27.4 us
  Pallas kernels: 0 us -> 84.2 us
  waiting for transfers between devices: 131 us -> 206 us
  other arithmetic: 45.5 us -> 11.5 us
  between operations: 14.1 us -> 0.89 us
  starting transfers between devices: 10.8 us -> 22.6 us
    all_gather x2, blocking collectives: 158 us -> 25.6 us  [the longest x1 16.8 us: shards_blocked(): serve_router = lax.all_gather(row_router, 'bank', axis=1, tiled=True)]
    all_to_all x2 -> x5, waiting for transfers between devices: 99.5 us -> 206 us  [the longest x4 199 us: shards_blocked(): lax.all_to_all(last, 'zero', split_axis=0, concat_axis=0, tiled=True)]
    pallas_call x0 -> x8, Pallas kernels: none -> 84.2 us  [the longest x4 45.8 us: prepare(): pl.pallas_call(functools.partial(prepare_kernel, parts), grid=(count,), i...]
    all_to_all x4 -> x0, local copies, waits for them, and re-layouts: 67.1 us -> none  [the longest x2 33.6 us: shards(): lax.all_to_all(narrow_gate, 'zero', split_axis=2, concat_axis=1, tiled=True)]
    psum x1 -> x0, waiting for transfers between devices: 31.5 us -> none  [shards(): lax.psum((jnp.sum(w_gate * w_gate, axis=1), jnp.sum(w_up * w_up, axis=1))...]
    unnamed x9 -> x22, local copies, waits for them, and re-layouts: 51.3 us -> 21.6 us
    convert_element_type x3 -> x0, other arithmetic: 28.3 us -> none  [the longest x1 14.1 us: shards(): (w_gate / jnp.expand_dims(scale_gate, 1)).astype(jnp.bfloat16)]
    all_to_all x2 -> x5, starting transfers between devices: 10.8 us -> 22.6 us  [the longest x4 17.4 us: shards_blocked(): lax.all_to_all(last, 'zero', split_axis=0, concat_axis=0, tiled=True)]
  transfers between devices with their start and end apart: 3 -> 5, of which waited for: 2 -> 4; matrix products, arithmetic and copies ran while one was open for 17% -> 2% of each run, Pallas kernels for 0% -> 20%
where the time goes in v1:
time: 380 us; the launch traced here: 378 us
  waiting for transfers between devices  206 us (54%)
  Pallas kernels  84.2 us (22%)
  local copies, waits for them, and re-layouts  27.4 us (7%)
  blocking collectives  25.6 us (7%)
  starting transfers between devices  22.6 us (6%)
  other arithmetic  11.5 us (3%)
    all_to_all x4, waiting for transfers between devices, shards_blocked(): lax.all_to_all(last, 'zero', split_axis=0, concat_axis=0, tiled=True)  199 us
    pallas_call x4, Pallas kernels, prepare(): pl.pallas_call(functools.partial(prepare_kernel, parts), grid=(count,), i...  45.8 us
    pallas_call x4, Pallas kernels, merge(): pl.pallas_call(functools.partial(merge_kernel, parts), grid=(count,), in_...  38.4 us
    unnamed x22, local copies, waits for them, and re-layouts  21.6 us
    all_to_all x4, starting transfers between devices, shards_blocked(): lax.all_to_all(last, 'zero', split_axis=0, concat_axis=0, tiled=True)  17.4 us
    all_gather x1, blocking collectives, shards_blocked(): serve_router = lax.all_gather(row_router, 'bank', axis=1, tiled=True)  16.8 us
    reduce_sum x1, other arithmetic, shards_blocked(): jnp.sum(w_up * w_up, axis=1)  9.5 us
    all_gather x1, blocking collectives, shards_blocked(): lax.all_gather(packed, 'zero', axis=0, tiled=True).reshape(parts, -1)  8.77 us
  transfers between devices with their start and end apart: 5, of which 4 were waited for; matrix products, arithmetic and copies ran while one was open for 2% of the time, Pallas kernels for 20%

profile of v1, /device:TPU:0, one launch (start us, length us, event | category | flops | bytes accessed | tf_op | source)
XLA Modules:
  0.0 377.8 jit_solution(9432781008010407562)
XLA Ops:
  0.6 9.5 %multiply_reduce_fusion = f32[32,768]{1,0:T(8,128)S(1)} fusion(f32[32,256,768]{2,1,0:T(8,128)} %w_ref.7), kind=kLoop, calls=%fused_computation | loop fusion | flops 12558336 | bytes 25264128 | tf_op jit(solution)/shard_map/reduce_sum | solution.py:79
  10.1 6.0 %copy-done.6 = f32[32,256,768]{2,1,0:T(8,128)S(1)} copy-done((f32[32,256,768]{2,1,0:T(8,128)S(1)}, f32[32,256,768]{2,1,0:T(8,128)}, u32[]{:S(2)}) %copy-start.6) | copy-done | bytes 25165848
  16.1 1.9 multiply_reduce_fusion.1
  19.0 5.2 %all-to-all-start = ((f32[8,64,96]{2,1,0:T(8,128)}), f32[8,64,96]{2,1,0:T(8,128)S(1)}, u32[]{:S(2)}, u32[]{:S(2)}) async-start(f32[8,64,96]{2,1,0:T(8,128)} %copy.19), calls=%async_computation | async-start | bytes 524288 | tf_op jit(solution)/shard_map/all_to_all | solution.py:81
  24.4 6.7 %all-to-all-done = f32[8,64,96]{2,1,0:T(8,128)S(1)} async-done(((f32[8,64,96]{2,1,0:T(8,128)}), f32[8,64,96]{2,1,0:T(8,128)S(1)}, u32[]{:S(2)}, u32[]{:S(2)}) %all-to-all-start) | async-done | bytes 196640 | tf_op jit(solution)/shard_map/all_to_all | solution.py:81
  31.2 8.8 %all_gather.6 = f32[8,112,128]{2,1,0:T(8,128)S(1)} all-gather(f32[1,112,128]{2,1,0:T(8,128)S(1)} %maximum_bitcast_fusion), channel_id=1, replica_groups=mesh['bank'=4,'zero'=8] {'zero'}, dimensions={0}, use_global_device_ids=true | all-gather | bytes 516096 | tf_op jit(solution)/shard_map/all_gather | solution.py:91
  40.2 0.8 copy-done.7
  41.4 5.8 %prepare.5 = bf16[8,8,96,256]{3,2,1,0:T(8,128)(2,1)S(1)} custom-call(f32[32,256,768]{2,1,0:T(8,128)} %w_ref.5, f32[32,1,768]{2,1,0:T(1,128)S(1)} %broadcast_in_dim.4.scale_ref), custom_call_target="tpu_custom_call" | custom-call | flops 62914560 | bytes 9437184 | tf_op jit(solution)/shard_map/prepare/pallas_call | solution.py:22
  47.2 1.7 copy-done.5
  48.9 3.7 all-to-all-start.2
  52.5 17.1 %prepare.4 = bf16[8,24,96,256]{3,2,1,0:T(8,128)(2,1)S(1)} custom-call(f32[32,256,768]{2,1,0:T(8,128)} %w_ref.5, f32[32,1,768]{2,1,0:T(1,128)S(1)} %broadcast_in_dim.4.scale_ref), custom_call_target="tpu_custom_call" | custom-call | flops 188743680 | bytes 28311552 | tf_op jit(solution)/shard_map/prepare/pallas_call | solution.py:22
  69.6 3.7 copy-done
  73.4 16.9 %all-to-all-done.2.block_ref = bf16[8,8,96,256]{3,2,1,0:T(8,128)(2,1)S(1)} async-done(((bf16[8,8,96,256]{3,2,1,0:T(8,128)(2,1)}), bf16[8,8,96,256]{3,2,1,0:T(8,128)(2,1)S(1)}, u32[]{:S(2)}, u32[]{:S(2)}) %all-to-all-start.2) | async-done | bytes 3145760 | tf_op jit(solution)/shard_map/all_to_all | solution.py:101
  90.3 5.1 %all-to-all-start.1 = ((bf16[8,24,96,256]{3,2,1,0:T(8,128)(2,1)}), bf16[8,24,96,256]{3,2,1,0:T(8,128)(2,1)}, u32[]{:S(2)}, u32[]{:S(2)}) async-start(bf16[8,24,96,256]{3,2,1,0:T(8,128)(2,1)} %copy-done), calls=%async_computation.1 | async-start | bytes 18874368 | tf_op jit(solution)/shard_map/all_to_all | solution.py:101
  95.6 17.1 %prepare.7 = bf16[8,24,96,256]{3,2,1,0:T(8,128)(2,1)S(1)} custom-call(f32[32,256,768]{2,1,0:T(8,128)} %w_ref.7, f32[32,1,768]{2,1,0:T(1,128)S(1)} %broadcast_in_dim.10.scale_ref), custom_call_target="tpu_custom_call" | custom-call | flops 188743680 | bytes 28311552 | tf_op jit(solution)/shard_map/prepare/pallas_call | solution.py:22
  112.7 3.7 copy-done.1
  116.5 84.2 %all-to-all-done.1.block_ref = bf16[8,24,96,256]{3,2,1,0:T(8,128)(2,1)} async-done(((bf16[8,24,96,256]{3,2,1,0:T(8,128)(2,1)}), bf16[8,24,96,256]{3,2,1,0:T(8,128)(2,1)}, u32[]{:S(2)}, u32[]{:S(2)}) %all-to-all-start.1) | async-done | bytes 9437216 | tf_op jit(solution)/shard_map/all_to_all | solution.py:101
  200.6 5.1 %all-to-all-start.4 = ((bf16[8,24,96,256]{3,2,1,0:T(8,128)(2,1)}), bf16[8,24,96,256]{3,2,1,0:T(8,128)(2,1)}, u32[]{:S(2)}, u32[]{:S(2)}) async-start(bf16[8,24,96,256]{3,2,1,0:T(8,128)(2,1)} %copy-done.1), calls=%async_computation.4 | async-start | bytes 18874368 | tf_op jit(solution)/shard_map/all_to_all | solution.py:101
  205.7 5.8 %prepare.6 = bf16[8,8,96,256]{3,2,1,0:T(8,128)(2,1)S(1)} custom-call(f32[32,256,768]{2,1,0:T(8,128)} %w_ref.7, f32[32,1,768]{2,1,0:T(1,128)S(1)} %broadcast_in_dim.10.scale_ref), custom_call_target="tpu_custom_call" | custom-call | flops 62914560 | bytes 9437184 | tf_op jit(solution)/shard_map/prepare/pallas_call | solution.py:22
  211.6 1.7 copy-done.4
  213.2 97.8 %all-to-all-done.4.block_ref = bf16[8,24,96,256]{3,2,1,0:T(8,128)(2,1)} async-done(((bf16[8,24,96,256]{3,2,1,0:T(8,128)(2,1)}), bf16[8,24,96,256]{3,2,1,0:T(8,128)(2,1)}, u32[]{:S(2)}, u32[]{:S(2)}) %all-to-all-start.4) | async-done | bytes 9437216 | tf_op jit(solution)/shard_map/all_to_all | solution.py:101
  311.0 3.6 all-to-all-start.3
  314.6 1.0 slice.34
  315.6 1.2 convert_element_type.9
  316.8 1.2 copy.23
  318.0 16.8 %all_gather.7 = bf16[2048,128]{0,1:T(8,128)(2,1)} all-gather(bf16[2048,32]{0,1:T(8,128)(2,1)S(1)} %copy.23), channel_id=1, replica_groups=mesh['bank'=4,'zero'=8] {'bank'}, dimensions={1}, use_global_device_ids=true | all-gather | bytes 655360 | tf_op jit(solution)/shard_map/all_gather | solution.py:106
  334.8 2.0 copy.24
  337.5 1.9 copy-done.3
  339.3 3.4 merge.4.refs_0_
  342.7 15.8 %merge.6.refs_0_ = bf16[32,96,2048]{2,1,0:T(8,128)(2,1)} custom-call(bf16[8,24,96,256]{3,2,1,0:T(8,128)(2,1)} %all-to-all-done.4.block_ref), custom_call_target="tpu_custom_call" | custom-call | flops 47185920 | bytes 18874368 | tf_op jit(solution)/shard_map/merge/pallas_call | solution.py:51
  358.5 15.8 %merge.5 = bf16[32,96,2048]{2,1,0:T(8,128)(2,1)} custom-call(bf16[8,24,96,256]{3,2,1,0:T(8,128)(2,1)} %all-to-all-done.1.block_ref, bf16[32,96,2048]{2,1,0:T(8,128)(2,1)} %merge.4.refs_0_), custom_call_target="tpu_custom_call", output_to_operand_aliasing={{}: (1, {})} | custom-call | flops 47185920 | bytes 18874368 | tf_op jit(solution)/shard_map/merge/pallas_call | solution.py:51
  374.4 3.4 merge.7
  (33 shorter events, 2.7 us)
Async XLA Ops:
  0.6 15.5 %copy-start.6 = (f32[32,256,768]{2,1,0:T(8,128)S(1)}, f32[32,256,768]{2,1,0:T(8,128)}, u32[]{:S(2)}) copy-start(f32[32,256,768]{2,1,0:T(8,128)} %w_ref.5) | copy-start | bytes 75497472
  16.1 8.1 %copy-start.8 = (f32[256,32]{0,1:T(8,128)S(1)}, f32[256,32]{0,1:T(8,128)}, u32[]{:S(2)}) copy-start(f32[256,32]{0,1:T(8,128)} %param.6) | copy-start | bytes 98308
  16.1 8.1 %copy-start.9 = (f32[256]{0:T(256)S(1)}, f32[256]{0:T(256)}, u32[]{:S(2)}) copy-start(f32[256]{0:T(256)} %param.7) | copy-start | bytes 3076
  19.0 12.1 %all-to-all-start = ((f32[8,64,96]{2,1,0:T(8,128)}), f32[8,64,96]{2,1,0:T(8,128)S(1)}, u32[]{:S(2)}, u32[]{:S(2)}) async-start(f32[8,64,96]{2,1,0:T(8,128)} %copy.19), calls=%async_computation | async-start | bytes 524288 | tf_op jit(solution)/shard_map/all_to_all | solution.py:81
  40.2 0.8 copy-start.7
  47.2 1.7 copy-start.5
  48.9 41.4 %all-to-all-start.2 = ((bf16[8,8,96,256]{3,2,1,0:T(8,128)(2,1)}), bf16[8,8,96,256]{3,2,1,0:T(8,128)(2,1)S(1)}, u32[]{:S(2)}, u32[]{:S(2)}) async-start(bf16[8,8,96,256]{3,2,1,0:T(8,128)(2,1)} %copy-done.5), calls=%async_computation.2 | async-start | bytes 6291456 | tf_op jit(solution)/shard_map/all_to_all | solution.py:101
  69.6 3.7 copy-start
  90.3 22.4 %copy-start.2 = (bf16[8,8,96,256]{3,2,1,0:T(8,128)(2,1)}, bf16[8,8,96,256]{3,2,1,0:T(8,128)(2,1)S(1)}, u32[]{:S(2)}) copy-start(bf16[8,8,96,256]{3,2,1,0:T(8,128)(2,1)S(1)} %all-to-all-done.2.block_ref) | copy-start | bytes 9437188
  90.3 110.3 %all-to-all-start.1 = ((bf16[8,24,96,256]{3,2,1,0:T(8,128)(2,1)}), bf16[8,24,96,256]{3,2,1,0:T(8,128)(2,1)}, u32[]{:S(2)}, u32[]{:S(2)}) async-start(bf16[8,24,96,256]{3,2,1,0:T(8,128)(2,1)} %copy-done), calls=%async_computation.1 | async-start | bytes 18874368 | tf_op jit(solution)/shard_map/all_to_all | solution.py:101
  112.7 3.7 copy-start.1
  200.6 110.3 %all-to-all-start.4 = ((bf16[8,24,96,256]{3,2,1,0:T(8,128)(2,1)}), bf16[8,24,96,256]{3,2,1,0:T(8,128)(2,1)}, u32[]{:S(2)}, u32[]{:S(2)}) async-start(bf16[8,24,96,256]{3,2,1,0:T(8,128)(2,1)} %copy-done.1), calls=%async_computation.4 | async-start | bytes 18874368 | tf_op jit(solution)/shard_map/all_to_all | solution.py:101
  211.6 1.7 copy-start.4
  311.0 63.4 %all-to-all-start.3 = ((bf16[8,8,96,256]{3,2,1,0:T(8,128)(2,1)}), bf16[8,8,96,256]{3,2,1,0:T(8,128)(2,1)S(1)}, u32[]{:S(2)}, u32[]{:S(2)}) async-start(bf16[8,8,96,256]{3,2,1,0:T(8,128)(2,1)} %copy-done.4), calls=%async_computation.3 | async-start | bytes 6291456 | tf_op jit(solution)/shard_map/all_to_all | solution.py:101
  337.4 1.9 copy-start.3

commit v2 on v1

--- a/solution.py
+++ b/solution.py
@@ -8,7 +8,8 @@
 from jax.sharding import PartitionSpec as P
 
 
-def prepare_kernel(parts, w_ref, scale_ref, out_ref):
+def prepare_kernel(parts, w_ref, scale_ref, *refs):
+    out_ref = refs[-1]
     normal = w_ref[0] / scale_ref[0]
     turned = normal.T
     width = turned.shape[0] // parts
@@ -16,7 +17,7 @@
         out_ref[part, 0] = turned[part * width : (part + 1) * width].astype(jnp.bfloat16)
 
 
-def prepare(w, scale, parts, first, count):
+def prepare(w, scale, parts, first, count, after):
     _, rows, columns = w.shape
     width = columns // parts
     return pl.pallas_call(
@@ -25,7 +26,8 @@
         in_specs=[
             pl.BlockSpec((1, rows, columns), lambda e: (e + first, 0, 0)),
             pl.BlockSpec((1, 1, columns), lambda e: (e + first, 0, 0)),
-        ],
+        ]
+        + [pl.BlockSpec(memory_space=pl.ANY)] * len(after),
         out_specs=pl.BlockSpec((parts, 1, width, rows), lambda e: (0, e, 0, 0)),
         out_shape=jax.ShapeDtypeStruct((parts, count, width, rows), jnp.bfloat16),
         cost_estimate=pl.CostEstimate(
@@ -33,13 +35,14 @@
             bytes_accessed=count * rows * columns * 6,
             transcendentals=0,
         ),
-        compiler_params=pltpu.CompilerParams(vmem_limit_bytes=32 * 2**20),
+        compiler_params=pltpu.CompilerParams(vmem_limit_bytes=56 * 2**20),
         name="prepare",
-    )(w, scale[:, None, :])
+    )(w, scale[:, None, :], *after)
 
 
 def merge_kernel(parts, block_ref, *refs):
-    out_ref = refs[-1]
+    out_ref, token_ref = refs[-2:]
+    token_ref[...] = jnp.zeros_like(token_ref)
     rows = block_ref.shape[3]
     for part in range(parts):
         out_ref[0, :, part * rows : (part + 1) * rows] = block_ref[part, 0]
@@ -53,21 +56,27 @@
         grid=(count,),
         in_specs=[pl.BlockSpec((parts, 1, width, rows), lambda e: (0, e, 0, 0))]
         + [pl.BlockSpec(memory_space=pl.ANY)] * chained,
-        out_specs=pl.BlockSpec((1, width, parts * rows), lambda e: (e + first, 0, 0)),
-        out_shape=jax.ShapeDtypeStruct((experts, width, parts * rows), jnp.bfloat16),
+        out_specs=[
+            pl.BlockSpec((1, width, parts * rows), lambda e: (e + first, 0, 0)),
+            pl.BlockSpec((8, 128), lambda e: (0, 0)),
+        ],
+        out_shape=[
+            jax.ShapeDtypeStruct((experts, width, parts * rows), jnp.bfloat16),
+            jax.ShapeDtypeStruct((8, 128), jnp.float32),
+        ],
         input_output_aliases={1: 0} if chained else {},
         cost_estimate=pl.CostEstimate(
             flops=count * rows * width * parts * 10,
             bytes_accessed=count * rows * width * parts * 4,
             transcendentals=0,
         ),
-        compiler_params=pltpu.CompilerParams(vmem_limit_bytes=32 * 2**20),
+        compiler_params=pltpu.CompilerParams(vmem_limit_bytes=56 * 2**20),
         name="merge",
     )(blocks, *([before] if chained else []))
 
 
 def cuts(experts, small_first):
-    small = max(experts // 4, 1)
+    small = max(experts * 3 // 16, 1)
     sizes = [small, experts - small] if small_first else [experts - small, small]
     return [size for size in sizes if size]
 
@@ -93,18 +102,27 @@
     scales = scales.transpose(1, 0, 2).reshape(2 * experts, columns)
     row_router = gathered[:, own.size :].reshape(parts * rows, -1).astype(jnp.bfloat16)
 
-    results, last = [], None
-    for w, scale, small_first in ((w_gate, scales[:experts], True), (w_up, scales[experts:], False)):
-        first, result = 0, None
-        for count in cuts(experts, small_first):
-            last = prepare(w, scale, parts, first, count)
-            blocks = lax.all_to_all(last, "zero", split_axis=0, concat_axis=0, tiled=True)
-            result = merge(blocks, result, experts, first)
-            first += count
-        results.append(result.transpose(0, 2, 1))
-    row_router, _ = lax.optimization_barrier((row_router, last))
-    serve_router = lax.all_gather(row_router, "bank", axis=1, tiled=True)
-    return (*results, scale_gate, scale_up, serve_router)
+    chunks = [(0, count) for count in cuts(experts, True)]
+    chunks += [(1, count) for count in cuts(experts, False)]
+    weights, scaled = (w_gate, w_up), (scales[:experts], scales[experts:])
+    first, results, tokens, serve_router = [0, 0], [None, None], [], None
+    for step, (which, count) in enumerate(chunks):
+        after = tokens[step - 2 : step - 1] if step >= 2 else []
+        if step == len(chunks) - 1:
+            row_router, *after = lax.optimization_barrier((row_router, *after))
+            serve_router = lax.all_gather(row_router, "bank", axis=1, tiled=True)
+            after = [*after, serve_router]
+        pieces = prepare(weights[which], scaled[which], parts, first[which], count, after)
+        blocks = lax.all_to_all(pieces, "zero", split_axis=0, concat_axis=0, tiled=True)
+        results[which], token = merge(blocks, results[which], experts, first[which])
+        tokens.append(token)
+        first[which] += count
+    return (
+        *(result.transpose(0, 2, 1) for result in results),
+        scale_gate,
+        scale_up,
+        serve_router,
+    )
 
 
 def shards_plain(w_gate, w_up, router_weight, router_gain):

time: 380 us -> 360 us (0.947)
  waiting for transfers between devices: 206 us -> 186 us
  local copies, waits for them, and re-layouts: 27.4 us -> 12.9 us
  Pallas kernels: 84.2 us -> 97.9 us
    all_to_all x4, waiting for transfers between devices: 199 us -> 180 us  [shards_blocked(): lax.all_to_all(pieces, 'zero', split_axis=0, concat_axis=0, tiled=True)]
    unnamed x22 -> x11, local copies, waits for them, and re-layouts: 21.6 us -> 7.56 us
    pallas_call x4, Pallas kernels: 45.8 us -> 53.9 us  [prepare(): pl.pallas_call(functools.partial(prepare_kernel, parts), grid=(count,), i...]
    reduce_sum x1, other arithmetic: 1.95 us -> 9.5 us  [shards_blocked(): jnp.sum(w_gate * w_gate, axis=1)]
    reduce_sum x1, other arithmetic: 9.5 us -> 1.95 us  [shards_blocked(): jnp.sum(w_up * w_up, axis=1)]
    pallas_call x4, Pallas kernels: 38.4 us -> 44 us  [merge(): pl.pallas_call(functools.partial(merge_kernel, parts), grid=(count,), in_...]
  transfers between devices with their start and end apart: 5 -> 5, of which waited for: 4 -> 5; matrix products, arithmetic and copies ran while one was open for 2% -> 1% of each run, Pallas kernels for 20% -> 24%
where the time goes in v2:
time: 360 us; the launch traced here: 357 us
  waiting for transfers between devices  186 us (52%)
  Pallas kernels  97.9 us (27%)
  blocking collectives  25.1 us (7%)
  starting transfers between devices  22.7 us (6%)
  local copies, waits for them, and re-layouts  12.9 us (4%)
  other arithmetic  11.5 us (3%)
    all_to_all x4, waiting for transfers between devices, shards_blocked(): lax.all_to_all(pieces, 'zero', split_axis=0, concat_axis=0, tiled=True)  180 us
    pallas_call x4, Pallas kernels, prepare(): pl.pallas_call(functools.partial(prepare_kernel, parts), grid=(count,), i...  53.9 us
    pallas_call x4, Pallas kernels, merge(): pl.pallas_call(functools.partial(merge_kernel, parts), grid=(count,), in_...  44 us
    all_to_all x4, starting transfers between devices, shards_blocked(): lax.all_to_all(pieces, 'zero', split_axis=0, concat_axis=0, tiled=True)  17.5 us
    all_gather x1, blocking collectives, shards_blocked(): serve_router = lax.all_gather(row_router, 'bank', axis=1, tiled=True)  16.3 us
    reduce_sum x1, other arithmetic, shards_blocked(): jnp.sum(w_gate * w_gate, axis=1)  9.5 us
    all_gather x1, blocking collectives, shards_blocked(): lax.all_gather(packed, 'zero', axis=0, tiled=True).reshape(parts, -1)  8.77 us
    unnamed x11, local copies, waits for them, and re-layouts  7.56 us
  transfers between devices with their start and end apart: 5, of which 5 were waited for; matrix products, arithmetic and copies ran while one was open for 1% of the time, Pallas kernels for 24%

profile of v2, /device:TPU:0, one launch (start us, length us, event | category | flops | bytes accessed | tf_op | source)
XLA Modules:
  0.0 357.1 jit_solution(18070718905446957507)
XLA Ops:
  0.6 9.5 %multiply_reduce_fusion.1 = f32[32,768]{1,0:T(8,128)S(1)} fusion(f32[32,256,768]{2,1,0:T(8,128)} %w_ref.5), kind=kLoop, calls=%fused_computation.1 | loop fusion | flops 12558336 | bytes 25264128 | tf_op jit(solution)/shard_map/reduce_sum | solution.py:88
  10.1 6.0 %copy-done = f32[32,256,768]{2,1,0:T(8,128)S(1)} copy-done((f32[32,256,768]{2,1,0:T(8,128)S(1)}, f32[32,256,768]{2,1,0:T(8,128)}, u32[]{:S(2)}) %copy-start) | copy-done | bytes 25165848
  16.1 1.9 multiply_reduce_fusion
  18.2 0.8 copy.20
  19.0 5.2 %all-to-all-start = ((f32[8,64,96]{2,1,0:T(8,128)}), f32[8,64,96]{2,1,0:T(8,128)S(1)}, u32[]{:S(2)}, u32[]{:S(2)}) async-start(f32[8,64,96]{2,1,0:T(8,128)} %copy.20), calls=%async_computation | async-start | bytes 524288 | tf_op jit(solution)/shard_map/all_to_all | solution.py:90
  24.4 6.7 %all-to-all-done = f32[8,64,96]{2,1,0:T(8,128)S(1)} async-done(((f32[8,64,96]{2,1,0:T(8,128)}), f32[8,64,96]{2,1,0:T(8,128)S(1)}, u32[]{:S(2)}, u32[]{:S(2)}) %all-to-all-start) | async-done | bytes 196640 | tf_op jit(solution)/shard_map/all_to_all | solution.py:90
  31.2 8.8 %all_gather.6 = f32[8,112,128]{2,1,0:T(8,128)S(1)} all-gather(f32[1,112,128]{2,1,0:T(8,128)S(1)} %maximum_bitcast_fusion), channel_id=1, replica_groups=mesh['bank'=4,'zero'=8] {'zero'}, dimensions={0}, use_global_device_ids=true | all-gather | bytes 516096 | tf_op jit(solution)/shard_map/all_gather | solution.py:100
  40.0 0.1 copy.29
  40.4 0.8 broadcast_in_dim.4.scale_ref
  41.2 5.8 %prepare.5 = bf16[8,6,96,256]{3,2,1,0:T(8,128)(2,1)} custom-call(f32[32,256,768]{2,1,0:T(8,128)} %w_ref.5, f32[32,1,768]{2,1,0:T(1,128)} %broadcast_in_dim.4.scale_ref), custom_call_target="tpu_custom_call" | custom-call | flops 47185920 | bytes 7077888 | tf_op jit(solution)/shard_map/prepare/pallas_call | solution.py:23
  47.0 3.6 %all-to-all-start.2 = ((bf16[8,6,96,256]{3,2,1,0:T(8,128)(2,1)}), bf16[8,6,96,256]{3,2,1,0:T(8,128)(2,1)S(1)}, u32[]{:S(2)}, u32[]{:S(2)}) async-start(bf16[8,6,96,256]{3,2,1,0:T(8,128)(2,1)} %prepare.5), calls=%async_computation.2 | async-start | bytes 4718592 | tf_op jit(solution)/shard_map/all_to_all | solution.py:116
  50.7 21.1 %prepare.4 = bf16[8,26,96,256]{3,2,1,0:T(8,128)(2,1)} custom-call(f32[32,256,768]{2,1,0:T(8,128)} %w_ref.5, f32[32,1,768]{2,1,0:T(1,128)} %broadcast_in_dim.4.scale_ref), custom_call_target="tpu_custom_call" | custom-call | flops 204472320 | bytes 30670848 | tf_op jit(solution)/shard_map/prepare/pallas_call | solution.py:23
  71.8 8.2 %all-to-all-done.2.block_ref = bf16[8,6,96,256]{3,2,1,0:T(8,128)(2,1)S(1)} async-done(((bf16[8,6,96,256]{3,2,1,0:T(8,128)(2,1)}), bf16[8,6,96,256]{3,2,1,0:T(8,128)(2,1)S(1)}, u32[]{:S(2)}, u32[]{:S(2)}) %all-to-all-start.2) | async-done | bytes 2359328 | tf_op jit(solution)/shard_map/all_to_all | solution.py:116
  80.0 5.1 %all-to-all-start.1 = ((bf16[8,26,96,256]{3,2,1,0:T(8,128)(2,1)}), bf16[8,26,96,256]{3,2,1,0:T(8,128)(2,1)}, u32[]{:S(2)}, u32[]{:S(2)}) async-start(bf16[8,26,96,256]{3,2,1,0:T(8,128)(2,1)} %prepare.4), calls=%async_computation.1 | async-start | bytes 20447232 | tf_op jit(solution)/shard_map/all_to_all | solution.py:116
  85.2 0.8 broadcast_in_dim.10.scale_ref
  86.1 4.9 %merge.4 = (bf16[32,96,2048]{2,1,0:T(8,128)(2,1)}, f32[8,128]{1,0:T(8,128)}) custom-call(bf16[8,6,96,256]{3,2,1,0:T(8,128)(2,1)} %copy-done.2), custom_call_target="tpu_custom_call" | custom-call | flops 11796480 | bytes 4718592 | tf_op jit(solution)/shard_map/merge/pallas_call | solution.py:54
  91.0 21.1 %prepare.7 = bf16[8,26,96,256]{3,2,1,0:T(8,128)(2,1)} custom-call(f32[32,256,768]{2,1,0:T(8,128)} %w_ref.7, f32[32,1,768]{2,1,0:T(1,128)} %broadcast_in_dim.10.scale_ref, f32[8,128]{1,0:T(8,128)} %get-tuple-element.18.refs_0_), custom_call_target="tpu_custom_call" | custom-call | flops 204472320 | bytes 30670848 | tf_op jit(solution)/shard_map/prepare/pallas_call | solution.py:23
  112.1 86.8 %all-to-all-done.1.block_ref = bf16[8,26,96,256]{3,2,1,0:T(8,128)(2,1)} async-done(((bf16[8,26,96,256]{3,2,1,0:T(8,128)(2,1)}), bf16[8,26,96,256]{3,2,1,0:T(8,128)(2,1)}, u32[]{:S(2)}, u32[]{:S(2)}) %all-to-all-start.1) | async-done | bytes 10223648 | tf_op jit(solution)/shard_map/all_to_all | solution.py:116
  198.9 5.2 %all-to-all-start.4 = ((bf16[8,26,96,256]{3,2,1,0:T(8,128)(2,1)}), bf16[8,26,96,256]{3,2,1,0:T(8,128)(2,1)}, u32[]{:S(2)}, u32[]{:S(2)}) async-start(bf16[8,26,96,256]{3,2,1,0:T(8,128)(2,1)} %prepare.7), calls=%async_computation.4 | async-start | bytes 20447232 | tf_op jit(solution)/shard_map/all_to_all | solution.py:116
  204.0 0.4 convert_element_type.9
  204.4 17.1 %merge.5 = (bf16[32,96,2048]{2,1,0:T(8,128)(2,1)}, f32[8,128]{1,0:T(8,128)}) custom-call(bf16[8,26,96,256]{3,2,1,0:T(8,128)(2,1)} %all-to-all-done.1.block_ref, bf16[32,96,2048]{2,1,0:T(8,128)(2,1)} %get-tuple-element.13.refs_0_), custom_call_target="tpu_custom_call", output_to_operand_aliasing={{0}: (1, {})} | custom-call | flops 51118080 | bytes 20447232 | tf_op jit(solution)/shard_map/merge/pallas_call | solution.py:54
  221.5 0.2 copy.24
  221.7 16.3 %all_gather.7 = bf16[2048,128]{0,1:T(8,128)(2,1)S(1)} all-gather(bf16[2048,32]{0,1:T(8,128)(2,1)S(1)} %copy.24), channel_id=1, replica_groups=mesh['bank'=4,'zero'=8] {'bank'}, dimensions={1}, use_global_device_ids=true | all-gather | bytes 655360 | tf_op jit(solution)/shard_map/all_gather | solution.py:113
  238.0 1.0 copy.25.refs_1_
  239.0 5.8 %prepare.6 = bf16[8,6,96,256]{3,2,1,0:T(8,128)(2,1)} custom-call(f32[32,256,768]{2,1,0:T(8,128)} %w_ref.7, f32[32,1,768]{2,1,0:T(1,128)} %broadcast_in_dim.10.scale_ref, f32[8,128]{1,0:T(8,128)} %get-tuple-element.16.refs_0_, bf16[2048,128]{1,0:T(8,128)(2,1)} %copy.25.refs_1_), custom_call_target="tpu_custom_call" | custom-call | flops 47185920 | bytes 7077888 | tf_op jit(solution)/shard_map/prepare/pallas_call | solution.py:23
  244.8 72.9 %all-to-all-done.4.block_ref = bf16[8,26,96,256]{3,2,1,0:T(8,128)(2,1)} async-done(((bf16[8,26,96,256]{3,2,1,0:T(8,128)(2,1)}), bf16[8,26,96,256]{3,2,1,0:T(8,128)(2,1)}, u32[]{:S(2)}, u32[]{:S(2)}) %all-to-all-start.4) | async-done | bytes 10223648 | tf_op jit(solution)/shard_map/all_to_all | solution.py:116
  317.7 3.6 %all-to-all-start.3 = ((bf16[8,6,96,256]{3,2,1,0:T(8,128)(2,1)}), bf16[8,6,96,256]{3,2,1,0:T(8,128)(2,1)S(1)}, u32[]{:S(2)}, u32[]{:S(2)}) async-start(bf16[8,6,96,256]{3,2,1,0:T(8,128)(2,1)} %prepare.6), calls=%async_computation.3 | async-start | bytes 4718592 | tf_op jit(solution)/shard_map/all_to_all | solution.py:116
  321.3 0.6 fusion.2
  322.0 17.1 %merge.6 = (bf16[32,96,2048]{2,1,0:T(8,128)(2,1)}, f32[8,128]{1,0:T(8,128)}) custom-call(bf16[8,26,96,256]{3,2,1,0:T(8,128)(2,1)} %all-to-all-done.4.block_ref), custom_call_target="tpu_custom_call" | custom-call | flops 51118080 | bytes 20447232 | tf_op jit(solution)/shard_map/merge/pallas_call | solution.py:54
  339.0 11.7 %all-to-all-done.3.block_ref = bf16[8,6,96,256]{3,2,1,0:T(8,128)(2,1)S(1)} async-done(((bf16[8,6,96,256]{3,2,1,0:T(8,128)(2,1)}), bf16[8,6,96,256]{3,2,1,0:T(8,128)(2,1)S(1)}, u32[]{:S(2)}, u32[]{:S(2)}) %all-to-all-start.3) | async-done | bytes 2359328 | tf_op jit(solution)/shard_map/all_to_all | solution.py:116
  350.7 1.4 copy-done.1
  352.1 4.9 %merge.7 = (bf16[32,96,2048]{2,1,0:T(8,128)(2,1)}, f32[8,128]{1,0:T(8,128)}) custom-call(bf16[8,6,96,256]{3,2,1,0:T(8,128)(2,1)} %copy-done.1, bf16[32,96,2048]{2,1,0:T(8,128)(2,1)} %get-tuple-element.19.refs_0_), custom_call_target="tpu_custom_call", output_to_operand_aliasing={{0}: (1, {})} | custom-call | flops 11796480 | bytes 4718592 | tf_op jit(solution)/shard_map/merge/pallas_call | solution.py:54
  (23 shorter events, 0.8 us)
Async XLA Ops:
  0.6 15.5 %copy-start = (f32[32,256,768]{2,1,0:T(8,128)S(1)}, f32[32,256,768]{2,1,0:T(8,128)}, u32[]{:S(2)}) copy-start(f32[32,256,768]{2,1,0:T(8,128)} %w_ref.7) | copy-start | bytes 75497472
  16.1 8.1 %copy-start.3 = (f32[256,32]{0,1:T(8,128)S(1)}, f32[256,32]{0,1:T(8,128)}, u32[]{:S(2)}) copy-start(f32[256,32]{0,1:T(8,128)} %param.6) | copy-start | bytes 98308
  16.1 8.1 %copy-start.4 = (f32[256]{0:T(256)S(1)}, f32[256]{0:T(256)}, u32[]{:S(2)}) copy-start(f32[256]{0:T(256)} %param.7) | copy-start | bytes 3076
  19.0 12.1 %all-to-all-start = ((f32[8,64,96]{2,1,0:T(8,128)}), f32[8,64,96]{2,1,0:T(8,128)S(1)}, u32[]{:S(2)}, u32[]{:S(2)}) async-start(f32[8,64,96]{2,1,0:T(8,128)} %copy.20), calls=%async_computation | async-start | bytes 524288 | tf_op jit(solution)/shard_map/all_to_all | solution.py:90
  47.0 33.0 %all-to-all-start.2 = ((bf16[8,6,96,256]{3,2,1,0:T(8,128)(2,1)}), bf16[8,6,96,256]{3,2,1,0:T(8,128)(2,1)S(1)}, u32[]{:S(2)}, u32[]{:S(2)}) async-start(bf16[8,6,96,256]{3,2,1,0:T(8,128)(2,1)} %prepare.5), calls=%async_computation.2 | async-start | bytes 4718592 | tf_op jit(solution)/shard_map/all_to_all | solution.py:116
  80.0 6.0 %copy-start.2 = (bf16[8,6,96,256]{3,2,1,0:T(8,128)(2,1)}, bf16[8,6,96,256]{3,2,1,0:T(8,128)(2,1)S(1)}, u32[]{:S(2)}) copy-start(bf16[8,6,96,256]{3,2,1,0:T(8,128)(2,1)S(1)} %all-to-all-done.2.block_ref) | copy-start | bytes 7077892
  80.0 118.8 %all-to-all-start.1 = ((bf16[8,26,96,256]{3,2,1,0:T(8,128)(2,1)}), bf16[8,26,96,256]{3,2,1,0:T(8,128)(2,1)}, u32[]{:S(2)}, u32[]{:S(2)}) async-start(bf16[8,26,96,256]{3,2,1,0:T(8,128)(2,1)} %prepare.4), calls=%async_computation.1 | async-start | bytes 20447232 | tf_op jit(solution)/shard_map/all_to_all | solution.py:116
  198.9 118.9 %all-to-all-start.4 = ((bf16[8,26,96,256]{3,2,1,0:T(8,128)(2,1)}), bf16[8,26,96,256]{3,2,1,0:T(8,128)(2,1)}, u32[]{:S(2)}, u32[]{:S(2)}) async-start(bf16[8,26,96,256]{3,2,1,0:T(8,128)(2,1)} %prepare.7), calls=%async_computation.4 | async-start | bytes 20447232 | tf_op jit(solution)/shard_map/all_to_all | solution.py:116
  317.7 33.0 %all-to-all-start.3 = ((bf16[8,6,96,256]{3,2,1,0:T(8,128)(2,1)}), bf16[8,6,96,256]{3,2,1,0:T(8,128)(2,1)S(1)}, u32[]{:S(2)}, u32[]{:S(2)}) async-start(bf16[8,6,96,256]{3,2,1,0:T(8,128)(2,1)} %prepare.6), calls=%async_computation.3 | async-start | bytes 4718592 | tf_op jit(solution)/shard_map/all_to_all | solution.py:116
  350.7 1.4 copy-start.1
